TPU v7x, 32 devices: a whole 2x2x4 slice. The times are simulated.
32 devices in a mesh: gx: 2 (over core), gyz: 16 (over z, y, x).
Axes of the slice: x: 2, y: 2, z: 4, core: 2. Of those that a mesh axis runs over, the one named last changes fastest.
Arguments:
- bands: bfloat16 [16, 80, 40, 512], P('gx', 'gyz'), may hold values from -6 to 6
- potential: float32 [16, 80, 40], P('gx', 'gyz'), may hold values from 0.5 to 4
- eigenvectors: bfloat16 [512, 512], P('gyz'), may hold values from -0.25 to 0.25
Outputs:
- correlation: float32 [512, 512], P('gyz')
- hamiltonian: float32 [512, 512], P('gyz')
- rotated: bfloat16 [16, 80, 40, 512], P('gx', 'gyz')
All inputs are finite; a program needn't handle non-finite values.
Results may differ from a plain program's by a relative error of at most 0.0012.
Values may be sent and summed in bfloat16 or wider, within the bound.
A program may use at most 64 MiB of HBM per device.

v0:
```python
import jax
import jax.numpy as jnp
from jax import lax
from jax.sharding import PartitionSpec as P


def extended(block, sides, width):
    for axis, dim in sides:
        count = lax.axis_size(axis)
        forward = [(i, i + 1) for i in range(count - 1)]
        backward = [(target, source) for source, target in forward]
        low = lax.ppermute(
            lax.slice_in_dim(block, block.shape[dim] - width, None, axis=dim), axis, forward
        )
        high = lax.ppermute(lax.slice_in_dim(block, 0, width, axis=dim), axis, backward)
        block = jnp.concatenate([low, block, high], axis=dim)
    return block


def stencil(padded, potential):
    centre = padded[1:-1, 1:-1, 1:-1].astype(jnp.float32)
    neighbours = padded[2:, 1:-1, 1:-1].astype(jnp.float32) + padded[:-2, 1:-1, 1:-1].astype(
        jnp.float32
    )
    neighbours = (
        neighbours
        + padded[1:-1, 2:, 1:-1].astype(jnp.float32)
        + padded[1:-1, :-2, 1:-1].astype(jnp.float32)
    )
    neighbours = (
        neighbours
        + padded[1:-1, 1:-1, 2:].astype(jnp.float32)
        + padded[1:-1, 1:-1, :-2].astype(jnp.float32)
    )
    return ((3.0 + potential[..., None]) * centre - 0.5 * neighbours).astype(jnp.bfloat16)


def on_device(bands, potential, eigenvectors):
    halo_bands = extended(bands, (("gx", 0), ("gyz", 1)), 1)
    padded = jnp.pad(halo_bands, ((0, 0), (0, 0), (1, 1), (0, 0)))
    hamil_bands = stencil(padded, potential)
    band_count = bands.shape[3]
    cell_count = bands.shape[0] * bands.shape[1] * bands.shape[2]
    flat_bands = bands.reshape(cell_count, band_count)
    combined = jnp.concatenate((flat_bands, hamil_bands.reshape(cell_count, band_count)), axis=1)
    inv_volume = 1.0 / (cell_count * lax.axis_size("gyz"))
    product = lax.dot_general(
        flat_bands, combined, (((0,), (0,)), ((), ())), preferred_element_type=jnp.float32
    )
    row_terms = lax.psum_scatter(product * inv_volume, "gyz", scatter_dimension=0, tiled=True)
    gram_block = lax.psum(row_terms, "gx")
    coefficients = lax.all_gather(eigenvectors, "gyz", axis=0, tiled=True)
    rotated = jnp.dot(flat_bands, coefficients, preferred_element_type=jnp.float32)
    return (
        gram_block[:, :band_count],
        gram_block[:, band_count:],
        rotated.astype(jnp.bfloat16).reshape(bands.shape),
    )


def solution(mesh):
    in_specs = (P("gx", "gyz", None, None), P("gx", "gyz", None), P("gyz", None))
    out_specs = (P("gyz", None), P("gyz", None), P("gx", "gyz", None, None))
    return jax.shard_map(
        on_device, mesh=mesh, in_specs=in_specs, out_specs=out_specs, check_vma=False
    )
```

profile of v0, /device:TPU:0, one launch (start us, length us, event | category | flops | bytes accessed | tf_op | source)
XLA Modules:
  0.0 162.3 jit_solution(2966103501217675455)
XLA Ops:
  7.2 0.0 reduce-scatter.4.cloned.1.call-start
  7.2 1.1 fusion.14
  8.3 2.4 %collective-permute-start.1 = (bf16[1,5,40,512]{3,2,1,0:T(8,128)(2,1)S(1)}, bf16[1,5,40,512]{3,2,1,0:T(8,128)(2,1)S(1)}, u32[]{:S(2)}, u32[]{:S(2)}) collective-permute-start(bf16[1,5,40,512]{3,2,1,0:T(8,128)(2,1)S(1)} %get-tuple-element.12), channel_id=1, source_target_pairs={{0,16},{1,17},{2,18},{3,19},{4,20},{5,21},{6,22},{7,23},{8,24},{9,... | collective-permute-start | bytes 614408 | tf_op jit(solution)/shard_map/ppermute | solution.py:12
  10.7 1.3 collective-permute-start
  12.0 0.0 collective-permute-done.1
  12.0 0.0 copy-start.2
  12.0 1.5 constant_dynamic-update-slice_fusion.1
  13.6 0.5 collective-permute-done
  14.1 0.1 fusion.13
  14.1 1.3 collective-permute-start.2
  15.4 4.9 %collective-permute-start.3 = (bf16[10,1,40,512]{3,2,1,0:T(8,128)(2,1)S(1)}, bf16[10,1,40,512]{3,2,1,0:T(8,128)(2,1)S(1)}, u32[]{:S(2)}, u32[]{:S(2)}) collective-permute-start(bf16[10,1,40,512]{3,2,1,0:T(8,128)(2,1)S(1)} %get-tuple-element.9), channel_id=1, source_target_pairs={{0,1},{1,2},{2,3},{3,4},{4,5},{5,6},{6,7},{7,8},{8,9},{9,10},{10,1... | collective-permute-start | bytes 1228808 | tf_op jit(solution)/shard_map/ppermute | solution.py:12
  20.3 0.0 copy-done.2
  20.3 0.0 copy-start
  20.3 8.3 %collective-permute-done.2 = bf16[10,1,40,512]{3,2,1,0:T(8,128)(2,1)S(1)} collective-permute-done((bf16[10,1,40,512]{3,2,1,0:T(8,128)(2,1)S(1)}, bf16[10,1,40,512]{3,2,1,0:T(8,128)(2,1)S(1)}, u32[]{:S(2)}, u32[]{:S(2)}) %collective-permute-start.2) | collective-permute-done | bytes 409632 | tf_op jit(solution)/shard_map/ppermute | solution.py:15
  28.6 9.9 %collective-permute-done.3 = bf16[10,1,40,512]{3,2,1,0:T(8,128)(2,1)S(1)} collective-permute-done((bf16[10,1,40,512]{3,2,1,0:T(8,128)(2,1)S(1)}, bf16[10,1,40,512]{3,2,1,0:T(8,128)(2,1)S(1)}, u32[]{:S(2)}, u32[]{:S(2)}) %collective-permute-start.3) | collective-permute-done | bytes 409632 | tf_op jit(solution)/shard_map/ppermute | solution.py:12
  38.6 1.7 %fusion.5 = bf16[10,7,42,512]{3,2,1,0:T(8,128)(2,1)S(1)} fusion(bf16[10,1,40,512]{3,2,1,0:T(8,128)(2,1)S(1)} %collective-permute-done.2, bf16[10,5,40,512]{3,2,1,0:T(8,128)(2,1)S(1)} %constant_dynamic-update-slice_fusion, bf16[10,1,40,512]{3,2,1,0:T(8,128)(2,1)S(1)} %collective-permute-done.3), kind=kLoop, calls=%fused_computation.7 | loop fusion | flops 18063360 | bytes 5877760 | tf_op jit(solution)/shard_map/concatenate | solution.py:16
  40.3 0.0 copy-done
  40.3 3.3 %subtract_convert_fusion = bf16[8,5,40,512]{3,2,1,0:T(8,128)(2,1)S(1)} fusion(bf16[8,5,40,512]{3,2,1,0:T(8,128)(2,1)S(1)} %copy-done, bf16[10,7,42,512]{3,2,1,0:T(8,128)(2,1)S(1)} %fusion.5, bf16[10,5,40,512]{3,2,1,0:T(8,128)(2,1)S(1)} %constant_dynamic-update-slice_fusion, bf16[10,1,40,512]{3,2,1,0:T(8,128)(2,1)S(1)} %collective-permute-done.3, ...), kind=kLoop, calls=%fused_computation.12 | loop fusion | flops 16384000 | bytes 9836800 | tf_op jit(solution)/shard_map/convert_element_type | solution.py:35
  43.6 3.4 %multiply_bitcast_fusion = f32[512,1024]{0,1:T(8,128)} fusion(bf16[1600,512]{1,0:T(8,128)(2,1)S(1)} %bitcast.9, bf16[1600,512]{1,0:T(8,128)(2,1)S(1)} %bitcast.11), kind=kOutput, calls=%fused_computation.14 | convolution fusion | flops 1684799488 | bytes 5373952 | tf_op jit(solution)/shard_map/dot_general | solution.py:47
  47.0 2.9 %copy.12 = f32[512,1024]{1,0:T(8,128)} copy(f32[512,1024]{0,1:T(8,128)} %multiply_bitcast_fusion) | data formatting | bytes 4194304
  50.0 0.0 reduce-scatter.4.cloned.1.call-update
  50.0 0.0 all-reduce.3.cloned.1.call-start
  50.0 0.7 copy-done.1
  50.7 46.1 %all_gather.3 = bf16[512,512]{1,0:T(8,128)(2,1)S(1)} all-gather(bf16[32,512]{1,0:T(8,128)(2,1)S(1)} %copy-done.1), channel_id=1, replica_groups=mesh['gx'=2,'gyz'=16] {'gyz'}, dimensions={0}, use_global_device_ids=true | all-gather | bytes 557056 | tf_op jit(solution)/shard_map/all_gather | solution.py:52
  96.9 36.3 %reduce-scatter.4.cloned.1.call-done = f32[32,1024]{1,0:T(8,128)} async-done(((f32[512,1024]{1,0:T(8,128)}), f32[32,1024]{1,0:T(8,128)}) %reduce-scatter.4.cloned.1.call-update) | async-done | bytes 131088
  133.1 1.9 %copy.13 = f32[32,1024]{0,1:T(8,128)} copy(f32[32,1024]{1,0:T(8,128)} %reduce-scatter.4.cloned.1.call-done) | data formatting | bytes 262144
  135.1 0.0 all-reduce.3.cloned.1.call-update
  135.1 2.2 %convolution_convert_fusion = bf16[1600,512]{1,0:T(8,128)(2,1)} fusion(bf16[1600,512]{1,0:T(8,128)(2,1)S(1)} %bitcast.10, bf16[512,512]{1,0:T(8,128)(2,1)S(1)} %all_gather.3), kind=kOutput, calls=%fused_computation.13 | convolution fusion | flops 839680000 | bytes 3801088 | tf_op jit(solution)/shard_map/dot_general | solution.py:53
  137.3 15.7 %all-reduce.3.cloned.1.call-done = f32[32,1024]{0,1:T(8,128)} async-done(((f32[32,1024]{0,1:T(8,128)}), f32[32,1024]{0,1:T(8,128)}) %all-reduce.3.cloned.1.call-update) | async-done | bytes 131088 | tf_op jit(solution)/shard_map/psum | solution.py:51
  152.9 1.1 fusion.15
  154.0 0.7 copy.10
  154.7 0.7 copy.11
  (5 shorter events, 0.0 us)
Async XLA Ops:
  7.2 126.0 %reduce-scatter.4.cloned.1.call-start = ((), (), s32[]{:S(2)}) async-start(), calls=%async_computation.2 | async-start | bytes 2228224
  8.3 3.7 %collective-permute-start.1 = (bf16[1,5,40,512]{3,2,1,0:T(8,128)(2,1)S(1)}, bf16[1,5,40,512]{3,2,1,0:T(8,128)(2,1)S(1)}, u32[]{:S(2)}, u32[]{:S(2)}) collective-permute-start(bf16[1,5,40,512]{3,2,1,0:T(8,128)(2,1)S(1)} %get-tuple-element.12), channel_id=1, source_target_pairs={{0,16},{1,17},{2,18},{3,19},{4,20},{5,21},{6,22},{7,23},{8,24},{9,... | collective-permute-start | bytes 614408 | tf_op jit(solution)/shard_map/ppermute | solution.py:12
  10.7 3.3 %collective-permute-start = (bf16[1,5,40,512]{3,2,1,0:T(8,128)(2,1)S(1)}, bf16[1,5,40,512]{3,2,1,0:T(8,128)(2,1)S(1)}, u32[]{:S(2)}, u32[]{:S(2)}) collective-permute-start(bf16[1,5,40,512]{3,2,1,0:T(8,128)(2,1)S(1)} %get-tuple-element.11), channel_id=1, source_target_pairs={{16,0},{17,1},{18,2},{19,3},{20,4},{21,5},{22,6},{23,7},{24,8},{25... | collective-permute-start | bytes 614408 | tf_op jit(solution)/shard_map/ppermute | solution.py:15
  12.0 8.3 %copy-start.2 = (f32[8,5,40]{2,0,1:T(8,128)S(1)}, f32[8,5,40]{2,0,1:T(8,128)}, u32[]{:S(2)}) copy-start(f32[8,5,40]{2,0,1:T(8,128)} %param.4) | copy-start | bytes 19204
  14.1 14.5 %collective-permute-start.2 = (bf16[10,1,40,512]{3,2,1,0:T(8,128)(2,1)S(1)}, bf16[10,1,40,512]{3,2,1,0:T(8,128)(2,1)S(1)}, u32[]{:S(2)}, u32[]{:S(2)}) collective-permute-start(bf16[10,1,40,512]{3,2,1,0:T(8,128)(2,1)S(1)} %get-tuple-element.10), channel_id=1, source_target_pairs={{1,0},{2,1},{3,2},{4,3},{5,4},{6,5},{7,6},{8,7},{9,8},{10,9},{11,1... | collective-permute-start | bytes 1228808 | tf_op jit(solution)/shard_map/ppermute | solution.py:15
  15.4 23.1 %collective-permute-start.3 = (bf16[10,1,40,512]{3,2,1,0:T(8,128)(2,1)S(1)}, bf16[10,1,40,512]{3,2,1,0:T(8,128)(2,1)S(1)}, u32[]{:S(2)}, u32[]{:S(2)}) collective-permute-start(bf16[10,1,40,512]{3,2,1,0:T(8,128)(2,1)S(1)} %get-tuple-element.9), channel_id=1, source_target_pairs={{0,1},{1,2},{2,3},{3,4},{4,5},{5,6},{6,7},{7,8},{8,9},{9,10},{10,1... | collective-permute-start | bytes 1228808 | tf_op jit(solution)/shard_map/ppermute | solution.py:12
  20.3 19.9 %copy-start = (bf16[8,5,40,512]{3,2,1,0:T(8,128)(2,1)S(1)}, bf16[8,5,40,512]{3,2,1,0:T(8,128)(2,1)}, u32[]{:S(2)}) copy-start(bf16[8,5,40,512]{3,2,1,0:T(8,128)(2,1)} %param.3) | copy-start | bytes 4915204
  50.0 0.8 copy-start.1
  50.0 102.9 %all-reduce.3.cloned.1.call-start = ((), (), s32[]{:S(2)}) async-start(), calls=%async_computation.1 | async-start | bytes 1048576 | tf_op jit(solution)/shard_map/psum | solution.py:51
Sparse Core Ops, SparseCore 0:
  50.1 82.9 reduce-scatter.3
  135.5 17.3 all-reduce.2
where the time goes:
time: 163 us; the launch traced here: 162 us
  waiting for transfers between devices  70.7 us (43%)
  blocking collectives  46.1 us (28%)
  between operations  14.2 us (9%)
  local copies, waits for them, and re-layouts  10.8 us (7%)
  starting transfers between devices  9.94 us (6%)
  matrix products  5.59 us (3%)
  other arithmetic  5.03 us (3%)
    all_gather x1, blocking collectives, on_device(): coefficients = lax.all_gather(eigenvectors, 'gyz', axis=0, tiled=True)  46.1 us
    unnamed x3, waiting for transfers between devices  36.3 us
    psum x1, waiting for transfers between devices, on_device(): gram_block = lax.psum(row_terms, 'gx')  15.7 us
    ppermute x2, waiting for transfers between devices, extended(): lax.ppermute(lax.slice_in_dim(block, block.shape[dim] - width, None, axis...  9.91 us
    ppermute x2, waiting for transfers between devices, extended(): lax.ppermute(lax.slice_in_dim(block, 0, width, axis=dim), axis, backward)  8.75 us
    unnamed x12, local copies, waits for them, and re-layouts  8.56 us
    ppermute x2, starting transfers between devices, extended(): lax.ppermute(lax.slice_in_dim(block, block.shape[dim] - width, None, axis...  7.28 us
    dot_general x1, matrix products, on_device(): lax.dot_general(flat_bands, combined, (((0,), (0,)), ((), ())), preferred...  3.41 us
  transfers between devices with their start and end apart: 6, of which 5 were waited for; matrix products, arithmetic and copies ran while one was open for 2% of the time, Pallas kernels for 0%

commit v1 on v0

--- a/solution.py
+++ b/solution.py
@@ -49,7 +49,12 @@
     )
     row_terms = lax.psum_scatter(product * inv_volume, "gyz", scatter_dimension=0, tiled=True)
     gram_block = lax.psum(row_terms, "gx")
-    coefficients = lax.all_gather(eigenvectors, "gyz", axis=0, tiled=True)
+    ring = [eigenvectors]
+    for hop in range(15):
+        ring.append(lax.ppermute(ring[-1], "gyz", [(dev, (dev + 1) % 16) for dev in range(16)]))
+    coefficients = jnp.roll(
+        jnp.concatenate(ring[::-1], axis=0), (lax.axis_index("gyz") + 1) * ring[0].shape[0], axis=0
+    )
     rotated = jnp.dot(flat_bands, coefficients, preferred_element_type=jnp.float32)
     return (
         gram_block[:, :band_count],

time: 163 us -> 193 us (1.18)
  waiting for transfers between devices: 70.7 us -> 144 us
  blocking collectives: 46.1 us -> 0 us
  starting transfers between devices: 9.94 us -> 12.4 us
    ppermute x0 -> x15, waiting for transfers between devices: none -> 113 us  [on_device(): lax.ppermute(ring[-1], 'gyz', [(dev, (dev + 1) % 16) for dev in range(16)])]
    all_gather x1 -> x0, blocking collectives: 46.1 us -> none  [on_device(): coefficients = lax.all_gather(eigenvectors, 'gyz', axis=0, tiled=True)]
    unnamed x3, waiting for transfers between devices: 36.3 us -> 0.05 us
    psum x1, waiting for transfers between devices: 15.7 us -> 12.4 us  [on_device(): gram_block = lax.psum(row_terms, 'gx')]
    ppermute x0 -> x15, starting transfers between devices: none -> 2.5 us  [on_device(): lax.ppermute(ring[-1], 'gyz', [(dev, (dev + 1) % 16) for dev in range(16)])]
    unnamed x12 -> x43, local copies, waits for them, and re-layouts: 8.56 us -> 8.68 us
  transfers between devices with their start and end apart: 6 -> 21, of which waited for: 5 -> 19; matrix products, arithmetic and copies ran while one was open for 2% -> 2% of each run, Pallas kernels for 0% -> 0%
where the time goes in v1:
time: 193 us; the launch traced here: 192 us
  waiting for transfers between devices  144 us (75%)
  between operations  14.4 us (7%)
  starting transfers between devices  12.4 us (6%)
  local copies, waits for them, and re-layouts  10.9 us (6%)
  matrix products  5.58 us (3%)
  other arithmetic  5.03 us (3%)
    ppermute x15, waiting for transfers between devices, on_device(): lax.ppermute(ring[-1], 'gyz', [(dev, (dev + 1) % 16) for dev in range(16)])  113 us
    psum x1, waiting for transfers between devices, on_device(): gram_block = lax.psum(row_terms, 'gx')  12.4 us
    ppermute x2, waiting for transfers between devices, extended(): lax.ppermute(lax.slice_in_dim(block, block.shape[dim] - width, None, axis...  9.91 us
    ppermute x2, waiting for transfers between devices, extended(): lax.ppermute(lax.slice_in_dim(block, 0, width, axis=dim), axis, backward)  8.75 us
    unnamed x43, local copies, waits for them, and re-layouts  8.68 us
    ppermute x2, starting transfers between devices, extended(): lax.ppermute(lax.slice_in_dim(block, block.shape[dim] - width, None, axis...  7.28 us
  transfers between devices with their start and end apart: 21, of which 19 were waited for; matrix products, arithmetic and copies ran while one was open for 2% of the time, Pallas kernels for 0%

profile of v1, /device:TPU:0, one launch (start us, length us, event | category | flops | bytes accessed | tf_op | source)
XLA Modules:
  0.0 192.3 jit_solution(14369486115781875179)
XLA Ops:
  7.2 1.1 fusion.16
  8.3 2.4 %collective-permute-start.1 = (bf16[1,5,40,512]{3,2,1,0:T(8,128)(2,1)S(1)}, bf16[1,5,40,512]{3,2,1,0:T(8,128)(2,1)S(1)}, u32[]{:S(2)}, u32[]{:S(2)}) collective-permute-start(bf16[1,5,40,512]{3,2,1,0:T(8,128)(2,1)S(1)} %get-tuple-element.12), channel_id=1, source_target_pairs={{0,16},{1,17},{2,18},{3,19},{4,20},{5,21},{6,22},{7,23},{8,24},{9,... | collective-permute-start | bytes 614408 | tf_op jit(solution)/shard_map/ppermute | solution.py:12
  10.7 1.3 collective-permute-start
  12.0 1.5 constant_dynamic-update-slice_fusion.1
  14.1 1.3 collective-permute-start.2
  15.4 4.9 %collective-permute-start.3 = (bf16[10,1,40,512]{3,2,1,0:T(8,128)(2,1)S(1)}, bf16[10,1,40,512]{3,2,1,0:T(8,128)(2,1)S(1)}, u32[]{:S(2)}, u32[]{:S(2)}) collective-permute-start(bf16[10,1,40,512]{3,2,1,0:T(8,128)(2,1)S(1)} %get-tuple-element.9), channel_id=1, source_target_pairs={{0,1},{1,2},{2,3},{3,4},{4,5},{5,6},{6,7},{7,8},{8,9},{9,10},{10,1... | collective-permute-start | bytes 1228808 | tf_op jit(solution)/shard_map/ppermute | solution.py:12
  20.3 8.3 %collective-permute-done.2 = bf16[10,1,40,512]{3,2,1,0:T(8,128)(2,1)S(1)} collective-permute-done((bf16[10,1,40,512]{3,2,1,0:T(8,128)(2,1)S(1)}, bf16[10,1,40,512]{3,2,1,0:T(8,128)(2,1)S(1)}, u32[]{:S(2)}, u32[]{:S(2)}) %collective-permute-start.2) | collective-permute-done | bytes 409632 | tf_op jit(solution)/shard_map/ppermute | solution.py:15
  28.6 9.9 %collective-permute-done.3 = bf16[10,1,40,512]{3,2,1,0:T(8,128)(2,1)S(1)} collective-permute-done((bf16[10,1,40,512]{3,2,1,0:T(8,128)(2,1)S(1)}, bf16[10,1,40,512]{3,2,1,0:T(8,128)(2,1)S(1)}, u32[]{:S(2)}, u32[]{:S(2)}) %collective-permute-start.3) | collective-permute-done | bytes 409632 | tf_op jit(solution)/shard_map/ppermute | solution.py:12
  38.6 1.7 fusion.5
  40.3 3.3 %subtract_convert_fusion = bf16[8,5,40,512]{3,2,1,0:T(8,128)(2,1)S(1)} fusion(bf16[8,5,40,512]{3,2,1,0:T(8,128)(2,1)S(1)} %copy-done, bf16[10,7,42,512]{3,2,1,0:T(8,128)(2,1)S(1)} %fusion.5, bf16[10,5,40,512]{3,2,1,0:T(8,128)(2,1)S(1)} %constant_dynamic-update-slice_fusion, bf16[10,1,40,512]{3,2,1,0:T(8,128)(2,1)S(1)} %collective-permute-done.3, ...), kind=kLoop, calls=%fused_computation.12 | loop fusion | flops 16384000 | bytes 9836800 | tf_op jit(solution)/shard_map/convert_element_type | solution.py:35
  43.6 3.4 %multiply_bitcast_fusion = f32[512,1024]{0,1:T(8,128)} fusion(bf16[1600,512]{1,0:T(8,128)(2,1)S(1)} %bitcast.10, bf16[1600,512]{1,0:T(8,128)(2,1)S(1)} %bitcast.12), kind=kOutput, calls=%fused_computation.14 | convolution fusion | flops 1684799488 | bytes 5373952 | tf_op jit(solution)/shard_map/dot_general | solution.py:47
  47.0 2.9 %copy.12 = f32[512,1024]{1,0:T(8,128)} copy(f32[512,1024]{0,1:T(8,128)} %multiply_bitcast_fusion) | data formatting | bytes 4194304
  50.7 2.5 %collective-permute-start.4 = (bf16[32,512]{1,0:T(8,128)(2,1)S(1)}, bf16[32,512]{1,0:T(8,128)(2,1)S(1)}, u32[]{:S(2)}, u32[]{:S(2)}) collective-permute-start(bf16[32,512]{1,0:T(8,128)(2,1)S(1)} %copy-done.1), channel_id=1, source_target_pairs={{0,1},{1,2},{2,3},{3,4},{4,5},{5,6},{6,7},{7,8},{8,9},{9,10},{10,1... | collective-permute-start | bytes 98312 | tf_op jit(solution)/shard_map/ppermute | solution.py:54
  53.1 5.0 %collective-permute-done.4 = bf16[32,512]{1,0:T(8,128)(2,1)S(1)} collective-permute-done((bf16[32,512]{1,0:T(8,128)(2,1)S(1)}, bf16[32,512]{1,0:T(8,128)(2,1)S(1)}, u32[]{:S(2)}, u32[]{:S(2)}) %collective-permute-start.4) | collective-permute-done | bytes 32800 | tf_op jit(solution)/shard_map/ppermute | solution.py:54
  58.2 7.7 %collective-permute-done.5 = bf16[32,512]{1,0:T(8,128)(2,1)S(1)} collective-permute-done((bf16[32,512]{1,0:T(8,128)(2,1)S(1)}, bf16[32,512]{1,0:T(8,128)(2,1)S(1)}, u32[]{:S(2)}, u32[]{:S(2)}) %collective-permute-start.5) | collective-permute-done | bytes 32800 | tf_op jit(solution)/shard_map/ppermute | solution.py:54
  65.9 7.9 %collective-permute-done.6 = bf16[32,512]{1,0:T(8,128)(2,1)S(1)} collective-permute-done((bf16[32,512]{1,0:T(8,128)(2,1)S(1)}, bf16[32,512]{1,0:T(8,128)(2,1)S(1)}, u32[]{:S(2)}, u32[]{:S(2)}) %collective-permute-start.6) | collective-permute-done | bytes 32800 | tf_op jit(solution)/shard_map/ppermute | solution.py:54
  73.9 7.6 %collective-permute-done.7 = bf16[32,512]{1,0:T(8,128)(2,1)S(1)} collective-permute-done((bf16[32,512]{1,0:T(8,128)(2,1)S(1)}, bf16[32,512]{1,0:T(8,128)(2,1)S(1)}, u32[]{:S(2)}, u32[]{:S(2)}) %collective-permute-start.7) | collective-permute-done | bytes 32800 | tf_op jit(solution)/shard_map/ppermute | solution.py:54
  81.5 7.5 %collective-permute-done.8 = bf16[32,512]{1,0:T(8,128)(2,1)S(1)} collective-permute-done((bf16[32,512]{1,0:T(8,128)(2,1)S(1)}, bf16[32,512]{1,0:T(8,128)(2,1)S(1)}, u32[]{:S(2)}, u32[]{:S(2)}) %collective-permute-start.8) | collective-permute-done | bytes 32800 | tf_op jit(solution)/shard_map/ppermute | solution.py:54
  89.0 8.2 %collective-permute-done.9 = bf16[32,512]{1,0:T(8,128)(2,1)S(1)} collective-permute-done((bf16[32,512]{1,0:T(8,128)(2,1)S(1)}, bf16[32,512]{1,0:T(8,128)(2,1)S(1)}, u32[]{:S(2)}, u32[]{:S(2)}) %collective-permute-start.9) | collective-permute-done | bytes 32800 | tf_op jit(solution)/shard_map/ppermute | solution.py:54
  97.2 7.9 %collective-permute-done.10 = bf16[32,512]{1,0:T(8,128)(2,1)S(1)} collective-permute-done((bf16[32,512]{1,0:T(8,128)(2,1)S(1)}, bf16[32,512]{1,0:T(8,128)(2,1)S(1)}, u32[]{:S(2)}, u32[]{:S(2)}) %collective-permute-start.10) | collective-permute-done | bytes 32800 | tf_op jit(solution)/shard_map/ppermute | solution.py:54
  105.0 7.5 %collective-permute-done.11 = bf16[32,512]{1,0:T(8,128)(2,1)S(1)} collective-permute-done((bf16[32,512]{1,0:T(8,128)(2,1)S(1)}, bf16[32,512]{1,0:T(8,128)(2,1)S(1)}, u32[]{:S(2)}, u32[]{:S(2)}) %collective-permute-start.11) | collective-permute-done | bytes 32800 | tf_op jit(solution)/shard_map/ppermute | solution.py:54
  112.6 7.9 %collective-permute-done.12 = bf16[32,512]{1,0:T(8,128)(2,1)S(1)} collective-permute-done((bf16[32,512]{1,0:T(8,128)(2,1)S(1)}, bf16[32,512]{1,0:T(8,128)(2,1)S(1)}, u32[]{:S(2)}, u32[]{:S(2)}) %collective-permute-start.12) | collective-permute-done | bytes 32800 | tf_op jit(solution)/shard_map/ppermute | solution.py:54
  120.5 7.5 %collective-permute-done.13 = bf16[32,512]{1,0:T(8,128)(2,1)S(1)} collective-permute-done((bf16[32,512]{1,0:T(8,128)(2,1)S(1)}, bf16[32,512]{1,0:T(8,128)(2,1)S(1)}, u32[]{:S(2)}, u32[]{:S(2)}) %collective-permute-start.13) | collective-permute-done | bytes 32800 | tf_op jit(solution)/shard_map/ppermute | solution.py:54
  128.0 7.5 %collective-permute-done.14 = bf16[32,512]{1,0:T(8,128)(2,1)S(1)} collective-permute-done((bf16[32,512]{1,0:T(8,128)(2,1)S(1)}, bf16[32,512]{1,0:T(8,128)(2,1)S(1)}, u32[]{:S(2)}, u32[]{:S(2)}) %collective-permute-start.14) | collective-permute-done | bytes 32800 | tf_op jit(solution)/shard_map/ppermute | solution.py:54
  135.5 7.5 %collective-permute-done.15 = bf16[32,512]{1,0:T(8,128)(2,1)S(1)} collective-permute-done((bf16[32,512]{1,0:T(8,128)(2,1)S(1)}, bf16[32,512]{1,0:T(8,128)(2,1)S(1)}, u32[]{:S(2)}, u32[]{:S(2)}) %collective-permute-start.15) | collective-permute-done | bytes 32800 | tf_op jit(solution)/shard_map/ppermute | solution.py:54
  143.0 7.8 %collective-permute-done.16 = bf16[32,512]{1,0:T(8,128)(2,1)S(1)} collective-permute-done((bf16[32,512]{1,0:T(8,128)(2,1)S(1)}, bf16[32,512]{1,0:T(8,128)(2,1)S(1)}, u32[]{:S(2)}, u32[]{:S(2)}) %collective-permute-start.16) | collective-permute-done | bytes 32800 | tf_op jit(solution)/shard_map/ppermute | solution.py:54
  150.9 7.5 %collective-permute-done.17 = bf16[32,512]{1,0:T(8,128)(2,1)S(1)} collective-permute-done((bf16[32,512]{1,0:T(8,128)(2,1)S(1)}, bf16[32,512]{1,0:T(8,128)(2,1)S(1)}, u32[]{:S(2)}, u32[]{:S(2)}) %collective-permute-start.17) | collective-permute-done | bytes 32800 | tf_op jit(solution)/shard_map/ppermute | solution.py:54
  158.4 7.5 %collective-permute-done.18 = bf16[32,512]{1,0:T(8,128)(2,1)S(1)} collective-permute-done((bf16[32,512]{1,0:T(8,128)(2,1)S(1)}, bf16[32,512]{1,0:T(8,128)(2,1)S(1)}, u32[]{:S(2)}, u32[]{:S(2)}) %collective-permute-start.18) | collective-permute-done | bytes 32800 | tf_op jit(solution)/shard_map/ppermute | solution.py:54
  166.3 1.9 copy.13
  168.3 2.2 %convolution_convert_fusion = bf16[512,1600]{0,1:T(8,128)(2,1)} fusion(bf16[1600,512]{1,0:T(8,128)(2,1)S(1)} %bitcast.11, bf16[1024,512]{1,0:T(8,128)(2,1)S(1)} %constant_dynamic-update-slice_fusion.3, s32[]{:T(128)S(6)} %select_n.14), kind=kOutput, calls=%fused_computation.13 | convolution fusion | flops 839680000 | bytes 3801092 | tf_op jit(solution)/shard_map/dot_general | solution.py:58
  170.4 12.4 %all-reduce.3.cloned.1.call-done = f32[32,1024]{0,1:T(8,128)} async-done(((f32[32,1024]{0,1:T(8,128)}), f32[32,1024]{0,1:T(8,128)}) %all-reduce.3.cloned.1.call-update) | async-done | bytes 131088 | tf_op jit(solution)/shard_map/psum | solution.py:51
  182.9 1.1 fusion.17
  (66 shorter events, 3.1 us)
Async XLA Ops:
  7.2 159.1 %reduce-scatter.4.cloned.1.call-start = ((), (), s32[]{:S(2)}) async-start(), calls=%async_computation.2 | async-start | bytes 2228224
  8.3 3.7 %collective-permute-start.1 = (bf16[1,5,40,512]{3,2,1,0:T(8,128)(2,1)S(1)}, bf16[1,5,40,512]{3,2,1,0:T(8,128)(2,1)S(1)}, u32[]{:S(2)}, u32[]{:S(2)}) collective-permute-start(bf16[1,5,40,512]{3,2,1,0:T(8,128)(2,1)S(1)} %get-tuple-element.12), channel_id=1, source_target_pairs={{0,16},{1,17},{2,18},{3,19},{4,20},{5,21},{6,22},{7,23},{8,24},{9,... | collective-permute-start | bytes 614408 | tf_op jit(solution)/shard_map/ppermute | solution.py:12
  10.7 3.3 %collective-permute-start = (bf16[1,5,40,512]{3,2,1,0:T(8,128)(2,1)S(1)}, bf16[1,5,40,512]{3,2,1,0:T(8,128)(2,1)S(1)}, u32[]{:S(2)}, u32[]{:S(2)}) collective-permute-start(bf16[1,5,40,512]{3,2,1,0:T(8,128)(2,1)S(1)} %get-tuple-element.11), channel_id=1, source_target_pairs={{16,0},{17,1},{18,2},{19,3},{20,4},{21,5},{22,6},{23,7},{24,8},{25... | collective-permute-start | bytes 614408 | tf_op jit(solution)/shard_map/ppermute | solution.py:15
  12.0 8.3 %copy-start.2 = (f32[8,5,40]{2,0,1:T(8,128)S(1)}, f32[8,5,40]{2,0,1:T(8,128)}, u32[]{:S(2)}) copy-start(f32[8,5,40]{2,0,1:T(8,128)} %param.4) | copy-start | bytes 19204
  14.1 14.5 %collective-permute-start.2 = (bf16[10,1,40,512]{3,2,1,0:T(8,128)(2,1)S(1)}, bf16[10,1,40,512]{3,2,1,0:T(8,128)(2,1)S(1)}, u32[]{:S(2)}, u32[]{:S(2)}) collective-permute-start(bf16[10,1,40,512]{3,2,1,0:T(8,128)(2,1)S(1)} %get-tuple-element.10), channel_id=1, source_target_pairs={{1,0},{2,1},{3,2},{4,3},{5,4},{6,5},{7,6},{8,7},{9,8},{10,9},{11,1... | collective-permute-start | bytes 1228808 | tf_op jit(solution)/shard_map/ppermute | solution.py:15
  15.4 23.1 %collective-permute-start.3 = (bf16[10,1,40,512]{3,2,1,0:T(8,128)(2,1)S(1)}, bf16[10,1,40,512]{3,2,1,0:T(8,128)(2,1)S(1)}, u32[]{:S(2)}, u32[]{:S(2)}) collective-permute-start(bf16[10,1,40,512]{3,2,1,0:T(8,128)(2,1)S(1)} %get-tuple-element.9), channel_id=1, source_target_pairs={{0,1},{1,2},{2,3},{3,4},{4,5},{5,6},{6,7},{7,8},{8,9},{9,10},{10,1... | collective-permute-start | bytes 1228808 | tf_op jit(solution)/shard_map/ppermute | solution.py:12
  20.3 19.9 %copy-start = (bf16[8,5,40,512]{3,2,1,0:T(8,128)(2,1)S(1)}, bf16[8,5,40,512]{3,2,1,0:T(8,128)(2,1)}, u32[]{:S(2)}) copy-start(bf16[8,5,40,512]{3,2,1,0:T(8,128)(2,1)} %param.3) | copy-start | bytes 4915204
  49.9 0.8 copy-start.1
  49.9 132.9 %all-reduce.3.cloned.1.call-start = ((), (), s32[]{:S(2)}) async-start(), calls=%async_computation.1 | async-start | bytes 1048576 | tf_op jit(solution)/shard_map/psum | solution.py:51
  50.7 7.5 %collective-permute-start.4 = (bf16[32,512]{1,0:T(8,128)(2,1)S(1)}, bf16[32,512]{1,0:T(8,128)(2,1)S(1)}, u32[]{:S(2)}, u32[]{:S(2)}) collective-permute-start(bf16[32,512]{1,0:T(8,128)(2,1)S(1)} %copy-done.1), channel_id=1, source_target_pairs={{0,1},{1,2},{2,3},{3,4},{4,5},{5,6},{6,7},{7,8},{8,9},{9,10},{10,1... | collective-permute-start | bytes 98312 | tf_op jit(solution)/shard_map/ppermute | solution.py:54
  58.2 7.8 %collective-permute-start.5 = (bf16[32,512]{1,0:T(8,128)(2,1)S(1)}, bf16[32,512]{1,0:T(8,128)(2,1)S(1)}, u32[]{:S(2)}, u32[]{:S(2)}) collective-permute-start(bf16[32,512]{1,0:T(8,128)(2,1)S(1)} %collective-permute-done.4), channel_id=1, source_target_pairs={{0,1},{1,2},{2,3},{3,4},{4,5},{5,6},{6,7},{7,8},{8,9},{9,10},{10,1... | collective-permute-start | bytes 98312 | tf_op jit(solution)/shard_map/ppermute | solution.py:54
  65.9 8.0 %collective-permute-start.6 = (bf16[32,512]{1,0:T(8,128)(2,1)S(1)}, bf16[32,512]{1,0:T(8,128)(2,1)S(1)}, u32[]{:S(2)}, u32[]{:S(2)}) collective-permute-start(bf16[32,512]{1,0:T(8,128)(2,1)S(1)} %collective-permute-done.5), channel_id=1, source_target_pairs={{0,1},{1,2},{2,3},{3,4},{4,5},{5,6},{6,7},{7,8},{8,9},{9,10},{10,1... | collective-permute-start | bytes 98312 | tf_op jit(solution)/shard_map/ppermute | solution.py:54
  73.9 7.6 %collective-permute-start.7 = (bf16[32,512]{1,0:T(8,128)(2,1)S(1)}, bf16[32,512]{1,0:T(8,128)(2,1)S(1)}, u32[]{:S(2)}, u32[]{:S(2)}) collective-permute-start(bf16[32,512]{1,0:T(8,128)(2,1)S(1)} %collective-permute-done.6), channel_id=1, source_target_pairs={{0,1},{1,2},{2,3},{3,4},{4,5},{5,6},{6,7},{7,8},{8,9},{9,10},{10,1... | collective-permute-start | bytes 98312 | tf_op jit(solution)/shard_map/ppermute | solution.py:54
  81.5 7.5 %collective-permute-start.8 = (bf16[32,512]{1,0:T(8,128)(2,1)S(1)}, bf16[32,512]{1,0:T(8,128)(2,1)S(1)}, u32[]{:S(2)}, u32[]{:S(2)}) collective-permute-start(bf16[32,512]{1,0:T(8,128)(2,1)S(1)} %collective-permute-done.7), channel_id=1, source_target_pairs={{0,1},{1,2},{2,3},{3,4},{4,5},{5,6},{6,7},{7,8},{8,9},{9,10},{10,1... | collective-permute-start | bytes 98312 | tf_op jit(solution)/shard_map/ppermute | solution.py:54
  89.0 8.2 %collective-permute-start.9 = (bf16[32,512]{1,0:T(8,128)(2,1)S(1)}, bf16[32,512]{1,0:T(8,128)(2,1)S(1)}, u32[]{:S(2)}, u32[]{:S(2)}) collective-permute-start(bf16[32,512]{1,0:T(8,128)(2,1)S(1)} %collective-permute-done.8), channel_id=1, source_target_pairs={{0,1},{1,2},{2,3},{3,4},{4,5},{5,6},{6,7},{7,8},{8,9},{9,10},{10,1... | collective-permute-start | bytes 98312 | tf_op jit(solution)/shard_map/ppermute | solution.py:54
  97.2 7.9 %collective-permute-start.10 = (bf16[32,512]{1,0:T(8,128)(2,1)S(1)}, bf16[32,512]{1,0:T(8,128)(2,1)S(1)}, u32[]{:S(2)}, u32[]{:S(2)}) collective-permute-start(bf16[32,512]{1,0:T(8,128)(2,1)S(1)} %collective-permute-done.9), channel_id=1, source_target_pairs={{0,1},{1,2},{2,3},{3,4},{4,5},{5,6},{6,7},{7,8},{8,9},{9,10},{10,1... | collective-permute-start | bytes 98312 | tf_op jit(solution)/shard_map/ppermute | solution.py:54
  105.0 7.5 %collective-permute-start.11 = (bf16[32,512]{1,0:T(8,128)(2,1)S(1)}, bf16[32,512]{1,0:T(8,128)(2,1)S(1)}, u32[]{:S(2)}, u32[]{:S(2)}) collective-permute-start(bf16[32,512]{1,0:T(8,128)(2,1)S(1)} %collective-permute-done.10), channel_id=1, source_target_pairs={{0,1},{1,2},{2,3},{3,4},{4,5},{5,6},{6,7},{7,8},{8,9},{9,10},{10,1... | collective-permute-start | bytes 98312 | tf_op jit(solution)/shard_map/ppermute | solution.py:54
  112.6 8.0 %collective-permute-start.12 = (bf16[32,512]{1,0:T(8,128)(2,1)S(1)}, bf16[32,512]{1,0:T(8,128)(2,1)S(1)}, u32[]{:S(2)}, u32[]{:S(2)}) collective-permute-start(bf16[32,512]{1,0:T(8,128)(2,1)S(1)} %collective-permute-done.11), channel_id=1, source_target_pairs={{0,1},{1,2},{2,3},{3,4},{4,5},{5,6},{6,7},{7,8},{8,9},{9,10},{10,1... | collective-permute-start | bytes 98312 | tf_op jit(solution)/shard_map/ppermute | solution.py:54
  120.5 7.5 %collective-permute-start.13 = (bf16[32,512]{1,0:T(8,128)(2,1)S(1)}, bf16[32,512]{1,0:T(8,128)(2,1)S(1)}, u32[]{:S(2)}, u32[]{:S(2)}) collective-permute-start(bf16[32,512]{1,0:T(8,128)(2,1)S(1)} %collective-permute-done.12), channel_id=1, source_target_pairs={{0,1},{1,2},{2,3},{3,4},{4,5},{5,6},{6,7},{7,8},{8,9},{9,10},{10,1... | collective-permute-start | bytes 98312 | tf_op jit(solution)/shard_map/ppermute | solution.py:54
  128.0 7.5 %collective-permute-start.14 = (bf16[32,512]{1,0:T(8,128)(2,1)S(1)}, bf16[32,512]{1,0:T(8,128)(2,1)S(1)}, u32[]{:S(2)}, u32[]{:S(2)}) collective-permute-start(bf16[32,512]{1,0:T(8,128)(2,1)S(1)} %collective-permute-done.13), channel_id=1, source_target_pairs={{0,1},{1,2},{2,3},{3,4},{4,5},{5,6},{6,7},{7,8},{8,9},{9,10},{10,1... | collective-permute-start | bytes 98312 | tf_op jit(solution)/shard_map/ppermute | solution.py:54
  135.5 7.5 %collective-permute-start.15 = (bf16[32,512]{1,0:T(8,128)(2,1)S(1)}, bf16[32,512]{1,0:T(8,128)(2,1)S(1)}, u32[]{:S(2)}, u32[]{:S(2)}) collective-permute-start(bf16[32,512]{1,0:T(8,128)(2,1)S(1)} %collective-permute-done.14), channel_id=1, source_target_pairs={{0,1},{1,2},{2,3},{3,4},{4,5},{5,6},{6,7},{7,8},{8,9},{9,10},{10,1... | collective-permute-start | bytes 98312 | tf_op jit(solution)/shard_map/ppermute | solution.py:54
  143.0 7.8 %collective-permute-start.16 = (bf16[32,512]{1,0:T(8,128)(2,1)S(1)}, bf16[32,512]{1,0:T(8,128)(2,1)S(1)}, u32[]{:S(2)}, u32[]{:S(2)}) collective-permute-start(bf16[32,512]{1,0:T(8,128)(2,1)S(1)} %collective-permute-done.15), channel_id=1, source_target_pairs={{0,1},{1,2},{2,3},{3,4},{4,5},{5,6},{6,7},{7,8},{8,9},{9,10},{10,1... | collective-permute-start | bytes 98312 | tf_op jit(solution)/shard_map/ppermute | solution.py:54
  150.9 7.5 %collective-permute-start.17 = (bf16[32,512]{1,0:T(8,128)(2,1)S(1)}, bf16[32,512]{1,0:T(8,128)(2,1)S(1)}, u32[]{:S(2)}, u32[]{:S(2)}) collective-permute-start(bf16[32,512]{1,0:T(8,128)(2,1)S(1)} %collective-permute-done.16), channel_id=1, source_target_pairs={{0,1},{1,2},{2,3},{3,4},{4,5},{5,6},{6,7},{7,8},{8,9},{9,10},{10,1... | collective-permute-start | bytes 98312 | tf_op jit(solution)/shard_map/ppermute | solution.py:54
  158.4 7.5 %collective-permute-start.18 = (bf16[32,512]{1,0:T(8,128)(2,1)S(1)}, bf16[32,512]{1,0:T(8,128)(2,1)S(1)}, u32[]{:S(2)}, u32[]{:S(2)}) collective-permute-start(bf16[32,512]{1,0:T(8,128)(2,1)S(1)} %collective-permute-done.17), channel_id=1, source_target_pairs={{0,1},{1,2},{2,3},{3,4},{4,5},{5,6},{6,7},{7,8},{8,9},{9,10},{10,1... | collective-permute-start | bytes 98312 | tf_op jit(solution)/shard_map/ppermute | solution.py:54
Sparse Core Ops, SparseCore 0:
  50.0 81.9 reduce-scatter.3
  168.4 14.4 all-reduce.2
